TPU v7x, 32 devices: a whole 2x2x4 slice. The times are simulated.
32 devices in a mesh: dp: 4 (over z), tp: 8 (over y, x, core).
Axes of the slice: x: 2, y: 2, z: 4, core: 2. Of those that a mesh axis runs over, the one named last changes fastest.
Arguments:
- w_up: bfloat16 [2, 2560, 10240], P(None, None, 'tp')
- w_down: bfloat16 [2, 10240, 2560], P(None, 'tp')
- x_saved: bfloat16 [2, 4, 2048, 2560], P(None, 'dp')
- h_saved: bfloat16 [2, 4, 2048, 10240], P(None, 'dp', None, 'tp')
- grad_out: bfloat16 [4, 2048, 2560], P('dp')
Outputs:
- output 1: bfloat16 [4, 2048, 2560], P('dp')
- output 2: float32 [2, 2560, 10240], P(None, None, 'tp')
- output 3: float32 [2, 10240, 2560], P(None, 'tp')
All inputs are finite; a program needn't handle non-finite values.
Results may differ from a plain program's by a relative error of at most 0.0130839.
Values are sent between devices in bfloat16 or wider.
A program may use at most 1 GiB of HBM per device.

v0:
```python
import jax
import jax.numpy as jnp
from jax import lax
from jax.sharding import PartitionSpec as P


def gelu_parts(hidden):
    tanh_val = jnp.tanh(0.7978845608028654 * (hidden + 0.044715 * hidden * hidden * hidden))
    gelu_out = 0.5 * hidden * (1.0 + tanh_val)
    gelu_slope = 0.5 * (1.0 + tanh_val) + 0.5 * hidden * (1.0 - tanh_val * tanh_val) * 0.7978845608028654 * (1.0 + 0.134145 * hidden * hidden)
    return gelu_out, gelu_slope


def solution(mesh):
    def run_backward(w_up, w_down, x_saved, h_saved, grad_out):
        layer_count = w_up.shape[0]
        grad_cur = grad_out
        up_grads = {}
        down_grads = {}
        for layer_idx in reversed(range(layer_count)):
            gelu_out, gelu_slope = gelu_parts(h_saved[layer_idx].astype(jnp.float32))
            act_grad = jnp.einsum("bsd,fd->bsf", grad_cur, w_down[layer_idx], preferred_element_type=jnp.float32)
            hid_grad = (act_grad * gelu_slope).astype(jnp.bfloat16)
            part_sum = jnp.einsum("bsf,df->bsd", hid_grad, w_up[layer_idx], preferred_element_type=jnp.float32).astype(jnp.bfloat16)
            full_sum = lax.psum(part_sum, "tp")
            down_grads[layer_idx] = jnp.einsum("bsf,bsd->fd", gelu_out.astype(jnp.bfloat16), grad_cur, preferred_element_type=jnp.float32)
            up_grads[layer_idx] = jnp.einsum("bsd,bsf->df", x_saved[layer_idx], hid_grad, preferred_element_type=jnp.float32)
            grad_cur = (grad_cur.astype(jnp.float32) + full_sum.astype(jnp.float32)).astype(jnp.bfloat16)
        up_total = lax.psum(jnp.stack([up_grads[layer_idx] for layer_idx in range(layer_count)]), "dp")
        down_total = lax.psum(jnp.stack([down_grads[layer_idx] for layer_idx in range(layer_count)]), "dp")
        return grad_cur, up_total, down_total
    return jax.shard_map(run_backward, mesh=mesh, in_specs=(P(None, None, "tp"), P(None, "tp", None), P(None, "dp", None, None), P(None, "dp", None, "tp"), P("dp", None, None)), out_specs=(P("dp", None, None), P(None, None, "tp"), P(None, "tp", None)), check_vma=False)
```

profile of v0, /device:TPU:0, one launch (start us, length us, event | category | flops | bytes accessed | tf_op | source)
XLA Modules:
  0.0 2185.3 jit_solution(9163268573010378632)
XLA Ops:
  7.2 0.0 all-reduce.5.cloned.1.call-start
  7.2 0.0 copy-start
  7.2 24.5 %fusion.21 = bf16[2048,1280]{1,0:T(8,128)(2,1)} fusion(bf16[1,2048,2560]{2,1,0:T(8,128)(2,1)} %param.9, bf16[2,1280,2560]{2,1,0:T(8,128)(2,1)} %param.6, bf16[2,1,2048,1280]{3,2,1,0:T(8,128)(2,1)} %param.8), kind=kOutput, calls=%fused_computation.43 | convolution fusion | flops 13474201600 | bytes 27525120 | tf_op jit(solution)/shard_map/bsd,fd->bsf/dot_general | solution.py:22
  31.7 0.0 copy-done
  31.7 18.5 fusion.56
  50.2 0.0 all-reduce.5.cloned.1.call-update
  50.2 0.3 all-reduce.7.cloned.1.call-start
  50.6 21.0 convolution_bitcast_fusion.2
  71.5 25.0 %convolution_bitcast_fusion = f32[1,1280,2560]{2,1,0:T(8,128)} fusion(bf16[1,2048,2560]{2,1,0:T(8,128)(2,1)} %param.9, bf16[2,1,2048,1280]{3,2,1,0:T(8,128)(2,1)} %param.8), kind=kOutput, calls=%fused_computation.30 | convolution fusion | flops 13447987200 | bytes 28835840 | tf_op jit(solution)/shard_map/bsf,bsd->fd/dot_general | solution.py:26
  96.5 105.3 %all-reduce.5.cloned.1.call-done = bf16[1,2048,2560]{2,1,0:T(8,128)(2,1)} async-done(((bf16[1,2048,2560]{2,1,0:T(8,128)(2,1)}), bf16[1,2048,2560]{2,1,0:T(8,128)(2,1)}) %all-reduce.5.cloned.1.call-update) | async-done | bytes 10485776 | tf_op jit(solution)/shard_map/psum | solution.py:25
  201.8 30.0 %fusion.35 = bf16[2048,1280]{1,0:T(8,128)(2,1)} fusion(bf16[2,1280,2560]{2,1,0:T(8,128)(2,1)} %param.6, bf16[2,1,2048,1280]{3,2,1,0:T(8,128)(2,1)} %param.8, bf16[1,2048,2560]{2,1,0:T(8,128)(2,1)} %all-reduce.5.cloned.1.call-done, bf16[1,2048,2560]{2,1,0:T(8,128)(2,1)} %param.9), kind=kOutput, calls=%fused_computation.57 | convolution fusion | flops 13495173120 | bytes 38010880 | tf_op jit(solution)/shard_map/bsd,fd->bsf/dot_general | solution.py:22
  231.8 20.1 fusion.57
  251.9 21.1 convolution_bitcast_fusion.3
  273.0 0.0 all-reduce.7.cloned.1.call-update
  273.0 0.0 all-reduce.9.cloned.1.call-start
  273.1 20.0 pad_maximum_fusion
  293.1 27.0 %convolution_bitcast_fusion.1 = f32[1,1280,2560]{2,1,0:T(8,128)} fusion(bf16[2,1,2048,1280]{3,2,1,0:T(8,128)(2,1)} %param.8, bf16[1,2048,2560]{2,1,0:T(8,128)(2,1)} %all-reduce.5.cloned.1.call-done, bf16[1,2048,2560]{2,1,0:T(8,128)(2,1)} %param.9), kind=kOutput, calls=%fused_computation.31 | convolution fusion | flops 13468958720 | bytes 39321600 | tf_op jit(solution)/shard_map/bsf,bsd->fd/dot_general | solution.py:26
  320.1 19.7 pad_maximum_fusion.1
  339.8 0.0 all-reduce.9.cloned.1.call-update
  339.9 82.0 %all-reduce.7.cloned.1.call-done = bf16[1,2048,2560]{2,1,0:T(8,128)(2,1)} async-done(((bf16[1,2048,2560]{2,1,0:T(8,128)(2,1)}), bf16[1,2048,2560]{2,1,0:T(8,128)(2,1)}) %all-reduce.7.cloned.1.call-update) | async-done | bytes 10485776 | tf_op jit(solution)/shard_map/psum | solution.py:25
  421.9 16.0 add_convert_fusion
  437.9 1695.5 %all-reduce.9.cloned.1.call-done = (f32[2,2560,1280]{1,2,0:T(8,128)}, f32[2,1280,2560]{2,1,0:T(8,128)}) async-done(((f32[2,2560,1280]{1,2,0:T(8,128)}, f32[2,1280,2560]{2,1,0:T(8,128)}), (f32[2,2560,1280]{1,2,0:T(8,128)}, f32[2,1280,2560]{2,1,0:T(8,128)})) %all-reduce.9.cloned.1.call-update) | async-done | bytes 52428816 | tf_op jit(solution)/shard_map/psum | solution.py:29
  2133.4 27.3 %copy.8 = f32[2,2560,1280]{2,1,0:T(8,128)} copy(f32[2,2560,1280]{1,2,0:T(8,128)} %get-tuple-element.6) | data formatting | bytes 52428800
  2160.7 17.6 copy.13
Async XLA Ops:
  7.2 194.6 %all-reduce.5.cloned.1.call-start = ((), (), s32[]{:S(2)}) async-start(), calls=%async_computation | async-start | bytes 20971520 | tf_op jit(solution)/shard_map/psum | solution.py:25
  7.2 24.5 %copy-start = (bf16[2,2560,1280]{2,1,0:T(8,128)(2,1)S(1)}, bf16[2,2560,1280]{2,1,0:T(8,128)(2,1)}, u32[]{:S(2)}) copy-start(bf16[2,2560,1280]{2,1,0:T(8,128)(2,1)} %param.5) | copy-start | bytes 39321604
  50.2 371.7 %all-reduce.7.cloned.1.call-start = ((), (), s32[]{:S(2)}) async-start(), calls=%async_computation.1 | async-start | bytes 20971520 | tf_op jit(solution)/shard_map/psum | solution.py:25
  273.0 1860.4 %all-reduce.9.cloned.1.call-start = ((), (), s32[]{:S(2)}) async-start(), calls=%async_computation.2 | async-start | bytes 104857600 | tf_op jit(solution)/shard_map/psum | solution.py:29
Sparse Core Ops, SparseCore 0:
  50.3 151.3 all-reduce.4
  273.2 148.7 all-reduce.6
  425.1 1708.2 all-reduce.8
where the time goes:
time: 2190 us
  waiting for transfers between devices  1880 us (86%)
  matrix products  187 us (9%)
  other arithmetic  55.7 us (3%)
  local copies, waits for them, and re-layouts  44.9 us (2%)
    psum x1, waiting for transfers between devices, run_backward(): lax.psum(jnp.stack([up_grads[layer_idx] for layer_idx in range(layer_coun...  1700 us
    psum x2, waiting for transfers between devices, run_backward(): full_sum = lax.psum(part_sum, 'tp')  187 us
    dot_general x2, matrix products, run_backward(): jnp.einsum('bsd,fd->bsf', grad_cur, w_down[layer_idx], preferred_element_...  54.5 us
    dot_general x2, matrix products, run_backward(): jnp.einsum('bsf,bsd->fd', gelu_out.astype(jnp.bfloat16), grad_cur, prefer...  52 us
    unnamed x4, local copies, waits for them, and re-layouts  44.9 us
  transfers between devices with their start and end apart: 3, of which 3 were waited for; matrix products, arithmetic and copies ran while one was open for 6% of the time, Pallas kernels for 0%

commit v1 on v0

v1 whole, which is shorter than its diff:
```python
import functools

import jax
import jax.numpy as jnp
from jax import lax
from jax.experimental import pallas as pl
from jax.experimental.pallas import tpu as pltpu
from jax.sharding import PartitionSpec as P

BF = jnp.bfloat16
F32 = jnp.float32
MESH = pl.DeviceIdType.MESH

N_DP = 4
N_TP = 8
def gelu_parts(hidden):
    sq = hidden * hidden
    tanh_val = jnp.tanh(0.7978845608028654 * (hidden + 0.044715 * sq * hidden))
    gelu_out = 0.5 * hidden * (1.0 + tanh_val)
    gelu_slope = 0.5 * (1.0 + tanh_val) + 0.5 * hidden * (1.0 - tanh_val * tanh_val) * 0.7978845608028654 * (1.0 + 0.134145 * sq)
    return gelu_out, gelu_slope


def dot_nn(a, b):
    return lax.dot_general(a, b, (((1,), (0,)), ((), ())), preferred_element_type=F32)


def dot_nt(a, b):
    return lax.dot_general(a, b, (((1,), (1,)), ((), ())), preferred_element_type=F32)


def dot_tn(a, b):
    return lax.dot_general(a, b, (((0,), (0,)), ((), ())), preferred_element_type=F32)


OWN = 4
HALF = 16
STEPS = 2 * HALF
ROUTES = {
    (1, 0, 0): ("", (1, 1, 4, 15)),
    (1, 0, 1): ("dx", (1, 7, 10, 8)),
    (1, 1, 0): ("dx", (5, 12, 11, 7)),
    (1, 1, 1): ("x", (1, 8, 4, 16)),
    (1, 2, 0): ("d", (11, 28, 22, 49)),
    (1, 2, 1): ("dx", (31, 38, 44, 44)),
    (1, 3, 1): ("x", (-1, 45, 45, 59)),
    (0, 0, 0): ("dx", (37, 75, 55, 25)),
    (0, 0, 1): ("", (51, 70, 69, 78)),
    (0, 1, 0): ("dx", (65, 71, 89, 93)),
    (0, 1, 1): ("dx", (71, 93, 89, 76)),
    (0, 2, 0): ("dx", (55, 72, 72, 86)),
    (0, 2, 1): ("dx", (101, 110, 110, 108)),
    (0, 3, 1): ("x", (-1, 114, 122, 124)),
}
Z_ORDER = ((0, 0), (1, 0), (0, 6), (1, 6))
X0_TICKS = (17, 12)
REDUCE = {1: 34, 0: 106}
MASKS = (0, 2, 4, 6)


def events_by_tick():
    found = {}
    for (blk, slot, arr), (_, at) in ROUTES.items():
        for mask, tick in zip(MASKS, at):
            if tick >= 0:
                found.setdefault(tick, []).append((blk, slot, arr, mask))
    for evs in found.values():
        evs.sort(key=lambda ev: ((ev[3] + 2) // 4, -ev[0], ev[1:]))
    return sorted(found.items())


def kernel(*refs):
    (w_up, w_dn, x_sv, h_sv, g_in, g_out, dw1, dw2, xg, gg, rsr, pair,
     w1, w2, acc1, acc2, xb, gb, hb, ab, dhb, pst, pcb, misc, x_sem, g_sem, h_sem, rs_pc, rs_own, recv, send) = refs

    part = gb.shape[0] // 2
    dim, hid = w1.shape
    z = lax.axis_index("dp")
    p = lax.axis_index("tp")
    bit_c, bit_x, bit_y = p % 2, (p // 2) % 2, p // 4

    def ident(mask):
        out = p
        if mask & 1:
            out = out + 1 - 2 * bit_c
        if mask & 2:
            out = out + 2 - 4 * bit_x
        if mask & 4:
            out = out + 4 - 8 * bit_y
        return out

    def flipped(flip_y, flip_x, flip_c):
        return ((bit_y + flip_y) % 2) * 4 + ((bit_x + flip_x) % 2) * 2 + (bit_c + flip_c) % 2

    def rows(idx):
        return pl.ds(pl.multiple_of(idx * part, part), part)

    def buf_slice(blk, slot, arr, mask):
        if slot == 3:
            return g_out.at[blk, rows(ident(mask)), :]
        return (xg, gg)[arr].at[blk, slot, rows(ident(mask)), :]

    def recv_idx(blk, slot, arr, mask):
        return ((blk * 4 + slot) * 2 + arr) * 8 + mask

    sent = []

    def remote(src, dst, where, rsem, cond=None):
        idx = len(sent)

        def make():
            return pltpu.make_async_remote_copy(src_ref=src(), dst_ref=dst(), send_sem=send.at[idx], recv_sem=rsem(), device_id=where(), device_id_type=MESH)

        sent.append((make, cond))
        if cond is None:
            make().start()
        else:
            pl.when(cond())(lambda: make().start())

    def wait_on(here, sem):
        pltpu.make_async_copy(here, here, sem).wait()

    def wait_arrival(*ev):
        wait_on(buf_slice(*ev), recv.at[recv_idx(*ev)])

    def forward(blk, slot, arr, mask, flip):
        remote(lambda: buf_slice(blk, slot, arr, mask), lambda: buf_slice(blk, slot, arr, mask), lambda: (z, ident(flip)), lambda: recv.at[recv_idx(blk, slot, arr, mask ^ flip)])

    def direct(blk, slot, arr):
        return "d" in ROUTES[blk, slot, arr][0]

    def is_end():
        return z % 3 == 0

    def is_inner():
        return z % 3 != 0

    def toward_middle():
        return z + 1 - 2 * (z // 2)

    def toward_end():
        return (z - 1 + 2 * (z // 2)) % N_DP

    def z_copy(src, blk, slot, arr, mask, dest, cond):
        if mask == 0 or direct(blk, slot, arr):
            remote(src, lambda: buf_slice(blk, slot, arr, mask), lambda: (dest(), p), lambda: recv.at[recv_idx(blk, slot, arr, mask)], cond)

    def z_send(blk, arr, mask):
        def src():
            whole = x_sv.at[blk] if arr == 0 else (g_in if blk == 1 else g_out.at[1])
            return whole.at[rows(ident(mask)), :]

        z_copy(src, blk, 0, arr, mask, toward_end, is_inner)
        z_copy(src, blk, 0, arr, mask, toward_middle, is_end)
        z_copy(src, blk, 1, arr, mask, toward_middle, is_inner)

    def send_on(blk, slot, arr, mask):
        first, second = (2, 4) if "x" in ROUTES[blk, slot, arr][0] else (4, 2)
        if slot < 3 and mask in (0, 6):
            where = (2, toward_middle) if slot == 0 else (slot, toward_end)
            z_copy(lambda: buf_slice(blk, slot, arr, mask), blk, where[0], arr, mask, where[1], is_inner)
        if mask == 0:
            forward(blk, slot, arr, 0, first)
            forward(blk, slot, arr, 0, second)
        elif mask == first and not direct(blk, slot, arr):
            forward(blk, slot, arr, first, second)
        forward(blk, slot, arr, mask, 1)
        if (blk, slot, mask) == (1, 3, 6):
            z_send(0, 1, 6)

    def halves(half):
        return pl.ds(half * part, part)

    def fetch(arr, step, dst, sem):
        at = step % HALF
        blk = 1 - step // HALF

        @pl.when(at < OWN)
        def _():
            for half in range(2):
                idx = flipped(at // 2, at % 2, half)
                if arr == 0:
                    pltpu.make_async_copy(x_sv.at[blk, rows(idx), :], dst(half), sem(half)).start()
                else:
                    @pl.when(blk == 1)
                    def _():
                        pltpu.make_async_copy(g_in.at[rows(idx), :], dst(half), sem(half)).start()

                    @pl.when(blk == 0)
                    def _():
                        here = g_out.at[1, rows(idx), :]
                        if half == 1:
                            wait_on(here, recv.at[recv_idx(1, 3, 1, 2 * at + 1)])
                        pltpu.make_async_copy(here, dst(half), sem(half)).start()

        @pl.when(at >= OWN)
        def _():
            slot = (at - OWN) // 4
            quarter = (at - OWN) % 4
            buf = (xg, gg)[arr]
            for half in range(2):
                here = buf.at[blk, slot, rows(flipped(quarter % 2, half, quarter // 2)), :]

                @pl.when(quarter >= 2)
                def _():
                    wait_on(here, recv.at[recv_idx(blk, slot, arr, 1 + 4 * (quarter % 2) + 2 * half)])

                pltpu.make_async_copy(here, dst(half), sem(half)).start()

    def x_dst(step):
        slot = step % 2
        return (lambda half: xb.at[slot, halves(half), :]), (lambda half: x_sem.at[slot * 2 + half])

    def g_dst():
        return (lambda half: gb.at[halves(half), :]), (lambda half: g_sem.at[half])

    def fetched(dst, sem):
        for half in range(2):
            wait_on(dst(half), sem(half))

    def h_fetch(step):
        at = step % HALF
        for half in range(2):
            pltpu.make_async_copy(h_sv.at[1 - step // HALF, rows(flipped(at // 2, at % 2, half)), :], hb.at[halves(half), :], h_sem.at[half]).start()

    def pair_copy(blk, at):
        return pltpu.make_async_remote_copy(src_ref=pst.at[halves(1), :], dst_ref=pcb.at[at % 2], send_sem=misc.at[0], recv_sem=rs_pc.at[blk * OWN + at], device_id=(z, ident(1)), device_id_type=MESH)

    chunk = 16

    def pair_sum(blk, at):
        wait_on(pcb.at[at % 2], rs_pc.at[blk * OWN + at])
        pair_copy(blk, at).wait_send()

        def add(r, carry):
            where = pl.ds(pl.multiple_of(r * chunk, chunk), chunk)
            pst[where, :] = (pst[where, :].astype(F32) + pcb[at % 2, where, :].astype(F32)).astype(BF)
            return carry

        lax.fori_loop(0, part // chunk, add, 0)
        copy = pltpu.make_async_copy(pst.at[halves(0), :], pair.at[blk, at], misc.at[1])
        copy.start()
        copy.wait()
        if at:
            remote(lambda: pair.at[blk, at], lambda: rsr.at[blk, at - 1], lambda: (z, ident(2 * at)), lambda: rs_own.at[blk * 3 + at - 1])

    def reduce_own(blk):
        for s in range(3):
            wait_on(rsr.at[blk, s], rs_own.at[blk * 3 + s])
        before = g_in if blk == 1 else g_out.at[1]
        loads = [
            pltpu.make_async_copy(pair.at[blk, 0], pst.at[halves(0), :], misc.at[1]),
            pltpu.make_async_copy(rsr.at[blk, 0], pst.at[halves(1), :], misc.at[2]),
            pltpu.make_async_copy(rsr.at[blk, 1], pcb.at[0], misc.at[3]),
            pltpu.make_async_copy(rsr.at[blk, 2], pcb.at[1], misc.at[4]),
            pltpu.make_async_copy(before.at[rows(p), :], gb.at[halves(0), :], misc.at[5]),
        ]
        for load in loads:
            load.start()
        for load in loads:
            load.wait()

        def add(r, carry):
            lo = pl.ds(pl.multiple_of(r * chunk, chunk), chunk)
            hi = pl.ds(pl.multiple_of(part + r * chunk, chunk), chunk)
            total = (pst[lo, :].astype(F32) + pst[hi, :].astype(F32)) + (pcb[0, lo, :].astype(F32) + pcb[1, lo, :].astype(F32))
            pst[lo, :] = (gb[lo, :].astype(F32) + total).astype(BF)
            return carry

        lax.fori_loop(0, part // chunk, add, 0)
        copy = pltpu.make_async_copy(pst.at[halves(0), :], g_out.at[blk, rows(p), :], misc.at[1])
        copy.start()
        copy.wait()
        send_on(blk, 3, 1, 0)
        if blk == 1:
            z_send(0, 1, 0)

    def ticks(step, point):
        for blk in (1, 0):
            if REDUCE[blk] % 4 == point:
                pl.when(step == REDUCE[blk] // 4)(functools.partial(reduce_own, blk))
        for mask, tick in zip((0, 6), X0_TICKS):
            if tick % 4 == point:
                pl.when(step == tick // 4)(functools.partial(z_send, 0, 0, mask))
        for tick, evs in events_by_tick():
            if tick % 4 == point:
                @pl.when(step == tick // 4)
                def _(evs=evs):
                    for ev in evs:
                        wait_arrival(*ev)
                        send_on(*ev)

    def load_w1(blk):
        return pltpu.make_async_copy(w_up.at[blk], w1, misc.at[2])

    def load_w2(blk):
        return pltpu.make_async_copy(w_dn.at[blk], w2, misc.at[3])

    def store_1(blk):
        return pltpu.make_async_copy(acc1, dw1.at[blk], misc.at[4])

    def store_2(blk):
        return pltpu.make_async_copy(acc2, dw2.at[blk], misc.at[5])

    def clear(ref):
        def some(r, carry):
            ref[pl.ds(pl.multiple_of(r * 16, 16), 16), :] = jnp.zeros((16, ref.shape[1]), F32)
            return carry

        lax.fori_loop(0, ref.shape[0] // 16, some, 0)

    load_w2(1).start()
    fetch(1, 0, *g_dst())
    h_fetch(0)
    fetch(0, 0, *x_dst(0))
    load_w1(1).start()
    for arr, mask in Z_ORDER:
        z_send(1, arr, mask)
    clear(acc2)
    clear(acc1)
    load_w2(1).wait()
    load_w1(1).wait()

    n_hid = 256
    n_dim = 512

    def hid_cols(j):
        return pl.ds(pl.multiple_of(j * n_hid, n_hid), n_hid)

    def dim_cols(j):
        return pl.ds(pl.multiple_of(j * n_dim, n_dim), n_dim)

    def step_body(step, carry):
        slot = step % 2
        at = step % HALF
        is_own = at < OWN
        ticks(step, 0)
        fetched(*x_dst(step))

        @pl.when(is_own)
        def _():
            for half in range(2):
                wait_on(hb.at[halves(half), :], h_sem.at[half])

        @pl.when(at >= OWN)
        def _():
            def h_part(j, c):
                hb[:, hid_cols(j)] = dot_nn(xb[slot], w1[:, hid_cols(j)]).astype(BF)
                return c

            lax.fori_loop(0, hid // n_hid, h_part, 0, unroll=True)

        ticks(step, 1)

        @pl.when(step == HALF - 1)
        def _():
            load_w1(0).start()

        @pl.when(step == HALF)
        def _():
            store_2(1).wait()
            clear(acc2)
            load_w2(0).wait()

        fetched(*g_dst())

        def a_part(j, c):
            act, slope = gelu_parts(hb[:, hid_cols(j)].astype(F32))
            ab[:, hid_cols(j)] = act.astype(BF)
            dhb[:, hid_cols(j)] = (dot_nt(gb[...], w2[hid_cols(j), :]) * slope).astype(BF)
            return c

        lax.fori_loop(0, hid // n_hid, a_part, 0, unroll=True)

        def down_part(j, c):
            acc2[hid_cols(j), :] += dot_tn(ab[:, hid_cols(j)], gb[...])
            return c

        lax.fori_loop(0, hid // n_hid, down_part, 0, unroll=True)

        @pl.when(step == HALF - 1)
        def _():
            load_w2(0).start()
            store_2(1).start()

        ticks(step, 2)

        @pl.when(step + 1 < STEPS)
        def _():
            fetch(0, step + 1, *x_dst(step + 1))
            fetch(1, step + 1, *g_dst())

        @pl.when((step + 1) % HALF < OWN)
        def _():
            pl.when(step + 1 < STEPS)(lambda: h_fetch(step + 1))

        for blk in (1, 0):
            for b in range(OWN):
                pl.when(step == (1 - blk) * HALF + b + 1)(functools.partial(pair_sum, blk, b))

        @pl.when(step == HALF)
        def _():
            load_w1(0).wait()

        @pl.when(is_own)
        def _():
            def p_part(j, c):
                pst[:, dim_cols(j)] = dot_nt(dhb[...], w1[dim_cols(j), :]).astype(BF)
                return c

            lax.fori_loop(0, dim // n_dim, p_part, 0, unroll=True)

        ticks(step, 3)
        for blk in (1, 0):
            for b in range(OWN):
                pl.when(step == (1 - blk) * HALF + b)(lambda blk=blk, b=b: pair_copy(blk, b).start())

        @pl.when(step == HALF)
        def _():
            store_1(1).wait()
            clear(acc1)

        def up_part(j, c):
            acc1[dim_cols(j), :] += dot_tn(xb[slot, :, dim_cols(j)], dhb[...])
            return c

        lax.fori_loop(0, dim // n_dim, up_part, 0, unroll=True)

        @pl.when(step == HALF - 1)
        def _():
            store_1(1).start()

        return carry

    lax.fori_loop(0, STEPS, step_body, 0)

    store_2(0).start()
    store_1(0).start()
    for mask in (1, 3, 5, 7):
        wait_arrival(0, 3, 1, mask)
    for make, cond in sent:
        if cond is None:
            make().wait_send()
        else:
            pl.when(cond())(lambda make=make: make().wait_send())
    store_2(0).wait()
    store_1(0).wait()


def backward(w_up, w_dn, x_sv, h_sv, g_in):
    _, dim, hid = w_up.shape
    tokens = g_in.shape[0]
    part = tokens // N_TP
    hbm = pl.BlockSpec(memory_space=pl.ANY)
    outs = [
        jax.ShapeDtypeStruct((2, tokens, dim), BF),
        jax.ShapeDtypeStruct((2, dim, hid), F32),
        jax.ShapeDtypeStruct((2, hid, dim), F32),
        jax.ShapeDtypeStruct((2, 3, tokens, dim), BF),
        jax.ShapeDtypeStruct((2, 3, tokens, dim), BF),
        jax.ShapeDtypeStruct((2, 3, part, dim), BF),
        jax.ShapeDtypeStruct((2, 4, part, dim), BF),
    ]
    dma = pltpu.SemaphoreType.DMA
    scratch = [
        pltpu.VMEM((dim, hid), BF),
        pltpu.VMEM((hid, dim), BF),
        pltpu.VMEM((dim, hid), F32),
        pltpu.VMEM((hid, dim), F32),
        pltpu.VMEM((2, 2 * part, dim), BF),
        pltpu.VMEM((2 * part, dim), BF),
        pltpu.VMEM((2 * part, hid), BF),
        pltpu.VMEM((2 * part, hid), BF),
        pltpu.VMEM((2 * part, hid), BF),
        pltpu.VMEM((2 * part, dim), BF),
        pltpu.VMEM((2, part, dim), BF),
        dma((6,)),
        dma((4,)),
        dma((2,)),
        dma((2,)),
        dma((2 * OWN,)),
        dma((6,)),
        dma((128,)),
        dma((176,)),
    ]
    return pl.pallas_call(
        kernel,
        out_shape=outs,
        in_specs=[hbm] * 5,
        out_specs=[hbm] * len(outs),
        scratch_shapes=scratch,
        compiler_params=pltpu.CompilerParams(has_side_effects=True, vmem_limit_bytes=67043328),
        cost_estimate=pl.CostEstimate(flops=STEPS * 4 * 4 * part * dim * hid, bytes_accessed=0, transcendentals=0),
        name="backward",
    )(w_up, w_dn, x_sv, h_sv, g_in)


def solution(mesh):
    def run_backward(w_up, w_down, x_saved, h_saved, grad_out):
        grads, up, down, *_ = backward(w_up, w_down, x_saved[:, 0], h_saved[:, 0], grad_out[0])
        return grads[:1], up, down

    return jax.shard_map(run_backward, mesh=mesh, in_specs=(P(None, None, "tp"), P(None, "tp", None), P(None, "dp", None, None), P(None, "dp", None, "tp"), P("dp", None, None)), out_specs=(P("dp", None, None), P(None, None, "tp"), P(None, "tp", None)), check_vma=False)
```

time: 2190 us -> 762 us (0.35)
  waiting for transfers between devices: 1880 us -> 0 us
  Pallas kernels: 0 us -> 719 us
  matrix products: 187 us -> 0 us
  other arithmetic: 55.7 us -> 0 us
    psum x3 -> x0, waiting for transfers between devices: 1880 us -> none  [the longest x1 1700 us: run_backward(): lax.psum(jnp.stack([up_grads[layer_idx] for layer_idx in range(layer_coun...]
    pallas_call x0 -> x1, Pallas kernels: none -> 719 us  [backward(): pl.pallas_call(kernel, out_shape=outs, in_specs=[hbm] * 5, out_specs=[hbm...]
    dot_general x8 -> x0, matrix products: 187 us -> none  [the longest x2 54.5 us: run_backward(): jnp.einsum('bsd,fd->bsf', grad_cur, w_down[layer_idx], preferred_element_...]
    another operation x2 -> x0, other arithmetic: 39.8 us -> none  [the longest x1 20 us: run_backward(): jnp.stack([up_grads[layer_idx] for layer_idx in range(layer_count)])]
  transfers between devices with their start and end apart: 3 -> 0, of which waited for: 3 -> 0; matrix products, arithmetic and copies ran while one was open for 6% -> 0% of each run, Pallas kernels for 0% -> 0%
where the time goes in v1:
time: 762 us
  Pallas kernels  719 us (94%)
  local copies, waits for them, and re-layouts  43.1 us (6%)
    pallas_call x1, Pallas kernels, backward(): pl.pallas_call(kernel, out_shape=outs, in_specs=[hbm] * 5, out_specs=[hbm...  719 us
    unnamed x4, local copies, waits for them, and re-layouts  34.3 us

profile of v1, /device:TPU:0, one launch (start us, length us, event | category | flops | bytes accessed | tf_op | source)
XLA Modules:
  0.0 762.3 jit_solution(6364172076677069673)
XLA Ops:
  0.6 718.6 %backward.1 = (bf16[2,2048,2560]{2,1,0:T(8,128)(2,1)}, f32[2,2560,1280]{2,1,0:T(8,128)}, f32[2,1280,2560]{2,1,0:T(8,128)}, bf16[2,3,2048,2560]{3,2,1,0:T(8,128)(...) custom-call(bf16[2,2560,1280]{2,1,0:T(8,128)(2,1)} %refs_0_.1, ...), custom_call_target="tpu_custom_call" | custom-call | flops 429496729600 | tf_op jit(solution)/shard_map/backward/pallas_call | solution.py:486
  719.2 8.7 %slice.3 = bf16[1,2048,2560]{2,1,0:T(8,128)(2,1)} slice(bf16[2,2048,2560]{2,1,0:T(8,128)(2,1)} %get-tuple-element.6), slice={[0:1], [0:2048], [0:2560]} | slice | bytes 20971520 | tf_op jit(solution)/shard_map/slice | solution.py:501
  727.9 0.0 copy-start
  727.9 18.6 %copy.10 = f32[2,2560,1280]{2,1,0:T(8,128)} copy(f32[2,2560,1280]{2,1,0:T(8,128)} %get-tuple-element.13) | data formatting | bytes 52428800
  746.5 6.5 copy-done
  753.0 9.3 %copy.11 = f32[2,1280,2560]{2,1,0:T(8,128)} copy(f32[2,1280,2560]{2,1,0:T(8,128)S(1)} %copy-done) | data formatting | bytes 52428800
Async XLA Ops:
  727.9 25.1 %copy-start = (f32[2,1280,2560]{2,1,0:T(8,128)S(1)}, f32[2,1280,2560]{2,1,0:T(8,128)}, u32[]{:S(2)}) copy-start(f32[2,1280,2560]{2,1,0:T(8,128)} %get-tuple-element.14) | copy-start | bytes 78643200

commit v2 on v1

--- a/solution.py
+++ b/solution.py
@@ -36,45 +36,51 @@
 OWN = 4
 HALF = 16
 STEPS = 2 * HALF
-ROUTES = {
-    (1, 0, 0): ("", (1, 1, 4, 15)),
-    (1, 0, 1): ("dx", (1, 7, 10, 8)),
-    (1, 1, 0): ("dx", (5, 12, 11, 7)),
-    (1, 1, 1): ("x", (1, 8, 4, 16)),
-    (1, 2, 0): ("d", (11, 28, 22, 49)),
-    (1, 2, 1): ("dx", (31, 38, 44, 44)),
-    (1, 3, 1): ("x", (-1, 45, 45, 59)),
-    (0, 0, 0): ("dx", (37, 75, 55, 25)),
-    (0, 0, 1): ("", (51, 70, 69, 78)),
-    (0, 1, 0): ("dx", (65, 71, 89, 93)),
-    (0, 1, 1): ("dx", (71, 93, 89, 76)),
-    (0, 2, 0): ("dx", (55, 72, 72, 86)),
-    (0, 2, 1): ("dx", (101, 110, 110, 108)),
-    (0, 3, 1): ("x", (-1, 114, 122, 124)),
-}
+SUB = 2
+KEYS = [(blk, slot, arr) for blk in (1, 0) for slot in range(4) for arr in range(2) if slot < 3 or arr == 1]
+ROUTES = (
+    ("x", "0103040d090c1214"),
+    ("dx", "0407080d0a100d14"),
+    ("dx", "0d151c1c17220f19"),
+    ("", "0c1114160d1b1522"),
+    ("d", "0e21162a162b3136"),
+    ("d", "152a2c2e2d2f2c35"),
+    ("x", "00002d2e2f324447"),
+    ("", "2d34323e3748434d"),
+    ("dx", "2e2e363a41454c51"),
+    ("dx", "3a514b5d565c435d"),
+    ("x", "3f52495a4c5b5366"),
+    ("d", "5769696e64726470"),
+    ("dx", "4d5f526953736b76"),
+    ("", "0000717d73777c7d"),
+)
 Z_ORDER = ((0, 0), (1, 0), (0, 6), (1, 6))
-X0_TICKS = (17, 12)
+X0_TICKS = (27, 4)
+COMBINE = {1: 26, 0: 94}
 REDUCE = {1: 34, 0: 106}
-MASKS = (0, 2, 4, 6)
+ROUTE = dict(zip(KEYS, ROUTES))
+PARTS = [(mask, sub) for mask in (0, 2, 4, 6) for sub in range(SUB)]
 
 
 def events_by_tick():
     found = {}
-    for (blk, slot, arr), (_, at) in ROUTES.items():
-        for mask, tick in zip(MASKS, at):
-            if tick >= 0:
-                found.setdefault(tick, []).append((blk, slot, arr, mask))
+    for (blk, slot, arr), (_, at) in ROUTE.items():
+        for (mask, sub), tick in zip(PARTS, bytes.fromhex(at)):
+            if slot < 3 or mask:
+                found.setdefault(tick, []).append((blk, slot, arr, mask, sub))
     for evs in found.values():
         evs.sort(key=lambda ev: ((ev[3] + 2) // 4, -ev[0], ev[1:]))
     return sorted(found.items())
 
 
 def kernel(*refs):
-    (w_up, w_dn, x_sv, h_sv, g_in, g_out, dw1, dw2, xg, gg, rsr, pair,
+    (w_up, w_dn, x_sv, h_sv, g_in, g_0, g_1, dw1, dw2, xg, gg, rsr, pair,
      w1, w2, acc1, acc2, xb, gb, hb, ab, dhb, pst, pcb, misc, x_sem, g_sem, h_sem, rs_pc, rs_own, recv, send) = refs
 
     part = gb.shape[0] // 2
+    small = part // SUB
     dim, hid = w1.shape
+    g_out = (g_0, g_1)
     z = lax.axis_index("dp")
     p = lax.axis_index("tp")
     bit_c, bit_x, bit_y = p % 2, (p // 2) % 2, p // 4
@@ -95,13 +101,22 @@
     def rows(idx):
         return pl.ds(pl.multiple_of(idx * part, part), part)
 
+    def sub_rows(idx, sub):
+        return pl.ds(pl.multiple_of(idx * part + sub * small, small), small)
+
+    def slice_at(blk, slot, arr, where):
+        if slot == 3:
+            return g_out[blk].at[where, :]
+        return (xg, gg)[arr].at[blk, slot, where, :]
+
+    def buf_part(blk, slot, arr, mask, sub):
+        return slice_at(blk, slot, arr, sub_rows(ident(mask), sub))
+
     def buf_slice(blk, slot, arr, mask):
-        if slot == 3:
-            return g_out.at[blk, rows(ident(mask)), :]
-        return (xg, gg)[arr].at[blk, slot, rows(ident(mask)), :]
-
-    def recv_idx(blk, slot, arr, mask):
-        return ((blk * 4 + slot) * 2 + arr) * 8 + mask
+        return slice_at(blk, slot, arr, rows(ident(mask)))
+
+    def recv_at(blk, slot, arr, mask, sub=0):
+        return recv.at[(((blk * 4 + slot) * 2 + arr) * 8 + mask) * SUB + sub]
 
     sent = []
 
@@ -120,14 +135,16 @@
     def wait_on(here, sem):
         pltpu.make_async_copy(here, here, sem).wait()
 
-    def wait_arrival(*ev):
-        wait_on(buf_slice(*ev), recv.at[recv_idx(*ev)])
-
-    def forward(blk, slot, arr, mask, flip):
-        remote(lambda: buf_slice(blk, slot, arr, mask), lambda: buf_slice(blk, slot, arr, mask), lambda: (z, ident(flip)), lambda: recv.at[recv_idx(blk, slot, arr, mask ^ flip)])
+    def forward(blk, slot, arr, mask, sub, flip):
+        here = lambda: buf_part(blk, slot, arr, mask, sub)
+        remote(here, here, lambda: (z, ident(flip)), lambda: recv_at(blk, slot, arr, mask ^ flip, sub))
+
+    def to_partner(blk, slot, arr, mask):
+        here = lambda: buf_slice(blk, slot, arr, mask)
+        remote(here, here, lambda: (z, ident(1)), lambda: recv_at(blk, slot, arr, mask ^ 1))
 
     def direct(blk, slot, arr):
-        return "d" in ROUTES[blk, slot, arr][0]
+        return "d" in ROUTE[blk, slot, arr][0]
 
     def is_end():
         return z % 3 == 0
@@ -141,32 +158,33 @@
     def toward_end():
         return (z - 1 + 2 * (z // 2)) % N_DP
 
-    def z_copy(src, blk, slot, arr, mask, dest, cond):
+    def z_copy(src, blk, slot, arr, mask, sub, dest, cond):
         if mask == 0 or direct(blk, slot, arr):
-            remote(src, lambda: buf_slice(blk, slot, arr, mask), lambda: (dest(), p), lambda: recv.at[recv_idx(blk, slot, arr, mask)], cond)
-
-    def z_send(blk, arr, mask):
+            remote(src, lambda: buf_part(blk, slot, arr, mask, sub), lambda: (dest(), p), lambda: recv_at(blk, slot, arr, mask, sub), cond)
+
+    def z_send(blk, arr, mask, sub):
         def src():
-            whole = x_sv.at[blk] if arr == 0 else (g_in if blk == 1 else g_out.at[1])
-            return whole.at[rows(ident(mask)), :]
-
-        z_copy(src, blk, 0, arr, mask, toward_end, is_inner)
-        z_copy(src, blk, 0, arr, mask, toward_middle, is_end)
-        z_copy(src, blk, 1, arr, mask, toward_middle, is_inner)
-
-    def send_on(blk, slot, arr, mask):
-        first, second = (2, 4) if "x" in ROUTES[blk, slot, arr][0] else (4, 2)
+            whole = x_sv.at[blk] if arr == 0 else (g_in if blk == 1 else g_1)
+            return whole.at[sub_rows(ident(mask), sub), :]
+
+        z_copy(src, blk, 0, arr, mask, sub, toward_end, is_inner)
+        z_copy(src, blk, 0, arr, mask, sub, toward_middle, is_end)
+        z_copy(src, blk, 1, arr, mask, sub, toward_middle, is_inner)
+
+    def send_on(blk, slot, arr, mask, sub):
+        first, second = (2, 4) if "x" in ROUTE[blk, slot, arr][0] else (4, 2)
         if slot < 3 and mask in (0, 6):
             where = (2, toward_middle) if slot == 0 else (slot, toward_end)
-            z_copy(lambda: buf_slice(blk, slot, arr, mask), blk, where[0], arr, mask, where[1], is_inner)
+            z_copy(lambda: buf_part(blk, slot, arr, mask, sub), blk, where[0], arr, mask, sub, where[1], is_inner)
         if mask == 0:
-            forward(blk, slot, arr, 0, first)
-            forward(blk, slot, arr, 0, second)
+            forward(blk, slot, arr, 0, sub, first)
+            forward(blk, slot, arr, 0, sub, second)
         elif mask == first and not direct(blk, slot, arr):
-            forward(blk, slot, arr, first, second)
-        forward(blk, slot, arr, mask, 1)
+            forward(blk, slot, arr, first, sub, second)
+        if sub == SUB - 1:
+            to_partner(blk, slot, arr, mask)
         if (blk, slot, mask) == (1, 3, 6):
-            z_send(0, 1, 6)
+            z_send(0, 1, 6, sub)
 
     def halves(half):
         return pl.ds(half * part, part)
@@ -188,9 +206,9 @@
 
                     @pl.when(blk == 0)
                     def _():
-                        here = g_out.at[1, rows(idx), :]
+                        here = g_1.at[rows(idx), :]
                         if half == 1:
-                            wait_on(here, recv.at[recv_idx(1, 3, 1, 2 * at + 1)])
+                            wait_on(here, recv_at(1, 3, 1, 2 * at + 1))
                         pltpu.make_async_copy(here, dst(half), sem(half)).start()
 
         @pl.when(at >= OWN)
@@ -199,11 +217,11 @@
             quarter = (at - OWN) % 4
             buf = (xg, gg)[arr]
             for half in range(2):
-                here = buf.at[blk, slot, rows(flipped(quarter % 2, half, quarter // 2)), :]
-
-                @pl.when(quarter >= 2)
+                here = buf.at[blk, slot, rows(flipped(quarter // 2, half, quarter % 2)), :]
+
+                @pl.when(quarter % 2 == 1)
                 def _():
-                    wait_on(here, recv.at[recv_idx(blk, slot, arr, 1 + 4 * (quarter % 2) + 2 * half)])
+                    wait_on(here, recv_at(blk, slot, arr, 1 + 4 * (quarter // 2) + 2 * half))
 
                 pltpu.make_async_copy(here, dst(half), sem(half)).start()
 
@@ -241,53 +259,94 @@
         copy = pltpu.make_async_copy(pst.at[halves(0), :], pair.at[blk, at], misc.at[1])
         copy.start()
         copy.wait()
-        if at:
-            remote(lambda: pair.at[blk, at], lambda: rsr.at[blk, at - 1], lambda: (z, ident(2 * at)), lambda: rs_own.at[blk * 3 + at - 1])
+        if at == 1:
+            p_send(blk, 1, 0, 0, 0)
+        if at == 2:
+            p_send(blk, 2, 1, 1, 1)
+        if at == 3:
+            p_send(blk, 3, 0, 2, 0)
+            p_send(blk, 3, 1, 2, 1)
+
+    def half_rows(low):
+        return pl.ds(low * (part // 2), part // 2)
+
+    def p_send(blk, src, low, dst, axis):
+        remote(lambda: pair.at[blk, src, half_rows(low), :], lambda: rsr.at[blk, dst, half_rows(low), :], lambda: (z, ident(2 + 2 * axis)), lambda: rs_own.at[blk * 6 + dst * 2 + low])
+
+    def p_wait(blk, dst):
+        for low in range(2):
+            wait_on(rsr.at[blk, dst, half_rows(low), :], rs_own.at[blk * 6 + dst * 2 + low])
+
+    def run_copies(copies):
+        for copy in copies:
+            copy.start()
+        for copy in copies:
+            copy.wait()
+
+    def combine(blk):
+        p_wait(blk, 2)
+        run_copies([
+            pltpu.make_async_copy(pair.at[blk, 2, half_rows(0), :], pst.at[half_rows(0), :], misc.at[1]),
+            pltpu.make_async_copy(pair.at[blk, 1, half_rows(1), :], pst.at[half_rows(1), :], misc.at[2]),
+            pltpu.make_async_copy(rsr.at[blk, 2], pcb.at[0], misc.at[3]),
+        ])
+
+        def add(r, carry):
+            lo = pl.ds(pl.multiple_of(r * chunk, chunk), chunk)
+            pst[lo, :] = (pst[lo, :].astype(F32) + pcb[0, lo, :].astype(F32)).astype(BF)
+            return carry
+
+        lax.fori_loop(0, part // chunk, add, 0)
+        run_copies([
+            pltpu.make_async_copy(pst.at[half_rows(0), :], pair.at[blk, 2, half_rows(0), :], misc.at[1]),
+            pltpu.make_async_copy(pst.at[half_rows(1), :], pair.at[blk, 1, half_rows(1), :], misc.at[2]),
+        ])
+        p_send(blk, 2, 0, 1, 1)
+        p_send(blk, 1, 1, 0, 0)
 
     def reduce_own(blk):
-        for s in range(3):
-            wait_on(rsr.at[blk, s], rs_own.at[blk * 3 + s])
-        before = g_in if blk == 1 else g_out.at[1]
-        loads = [
+        p_wait(blk, 0)
+        p_wait(blk, 1)
+        before = g_in if blk == 1 else g_1
+        run_copies([
             pltpu.make_async_copy(pair.at[blk, 0], pst.at[halves(0), :], misc.at[1]),
             pltpu.make_async_copy(rsr.at[blk, 0], pst.at[halves(1), :], misc.at[2]),
             pltpu.make_async_copy(rsr.at[blk, 1], pcb.at[0], misc.at[3]),
-            pltpu.make_async_copy(rsr.at[blk, 2], pcb.at[1], misc.at[4]),
             pltpu.make_async_copy(before.at[rows(p), :], gb.at[halves(0), :], misc.at[5]),
-        ]
-        for load in loads:
-            load.start()
-        for load in loads:
-            load.wait()
+        ])
 
         def add(r, carry):
             lo = pl.ds(pl.multiple_of(r * chunk, chunk), chunk)
             hi = pl.ds(pl.multiple_of(part + r * chunk, chunk), chunk)
-            total = (pst[lo, :].astype(F32) + pst[hi, :].astype(F32)) + (pcb[0, lo, :].astype(F32) + pcb[1, lo, :].astype(F32))
+            total = pst[lo, :].astype(F32) + pst[hi, :].astype(F32) + pcb[0, lo, :].astype(F32)
             pst[lo, :] = (gb[lo, :].astype(F32) + total).astype(BF)
             return carry
 
         lax.fori_loop(0, part // chunk, add, 0)
-        copy = pltpu.make_async_copy(pst.at[halves(0), :], g_out.at[blk, rows(p), :], misc.at[1])
-        copy.start()
-        copy.wait()
-        send_on(blk, 3, 1, 0)
+        run_copies([pltpu.make_async_copy(pst.at[halves(0), :], g_out[blk].at[rows(p), :], misc.at[1])])
+        for sub in range(SUB):
+            send_on(blk, 3, 1, 0, sub)
         if blk == 1:
-            z_send(0, 1, 0)
+            for sub in range(SUB):
+                z_send(0, 1, 0, sub)
 
     def ticks(step, point):
         for blk in (1, 0):
-            if REDUCE[blk] % 4 == point:
-                pl.when(step == REDUCE[blk] // 4)(functools.partial(reduce_own, blk))
+            for when, act in ((COMBINE, combine), (REDUCE, reduce_own)):
+                if when[blk] % 4 == point:
+                    pl.when(step == when[blk] // 4)(functools.partial(act, blk))
         for mask, tick in zip((0, 6), X0_TICKS):
             if tick % 4 == point:
-                pl.when(step == tick // 4)(functools.partial(z_send, 0, 0, mask))
+                @pl.when(step == tick // 4)
+                def _(mask=mask):
+                    for sub in range(SUB):
+                        z_send(0, 0, mask, sub)
         for tick, evs in events_by_tick():
             if tick % 4 == point:
                 @pl.when(step == tick // 4)
                 def _(evs=evs):
                     for ev in evs:
-                        wait_arrival(*ev)
+                        wait_on(buf_part(*ev), recv_at(*ev))
                         send_on(*ev)
 
     def load_w1(blk):
@@ -315,7 +374,8 @@
     fetch(0, 0, *x_dst(0))
     load_w1(1).start()
     for arr, mask in Z_ORDER:
-        z_send(1, arr, mask)
+        for sub in range(SUB):
+            z_send(1, arr, mask, sub)
     clear(acc2)
     clear(acc1)
     load_w2(1).wait()
@@ -342,19 +402,7 @@
             for half in range(2):
                 wait_on(hb.at[halves(half), :], h_sem.at[half])
 
-        @pl.when(at >= OWN)
-        def _():
-            def h_part(j, c):
-                hb[:, hid_cols(j)] = dot_nn(xb[slot], w1[:, hid_cols(j)]).astype(BF)
-                return c
-
-            lax.fori_loop(0, hid // n_hid, h_part, 0, unroll=True)
-
         ticks(step, 1)
-
-        @pl.when(step == HALF - 1)
-        def _():
-            load_w1(0).start()
 
         @pl.when(step == HALF)
         def _():
@@ -364,24 +412,42 @@
 
         fetched(*g_dst())
 
-        def a_part(j, c):
+        def a_part(j):
             act, slope = gelu_parts(hb[:, hid_cols(j)].astype(F32))
             ab[:, hid_cols(j)] = act.astype(BF)
             dhb[:, hid_cols(j)] = (dot_nt(gb[...], w2[hid_cols(j), :]) * slope).astype(BF)
-            return c
-
-        lax.fori_loop(0, hid // n_hid, a_part, 0, unroll=True)
-
-        def down_part(j, c):
-            acc2[hid_cols(j), :] += dot_tn(ab[:, hid_cols(j)], gb[...])
-            return c
-
-        lax.fori_loop(0, hid // n_hid, down_part, 0, unroll=True)
+
+
+        def h_part(j):
+            hb[:, hid_cols(j)] = dot_nn(xb[slot], w1[:, hid_cols(j)]).astype(BF)
+
+        def down():
+            acc2[...] += dot_tn(ab[...], gb[...])
+
+        @pl.when(is_own)
+        def _():
+            for j in range(hid // n_hid):
+                a_part(j)
+            down()
+
+        @pl.when(at >= OWN)
+        def _():
+            h_part(0)
+            for j in range(hid // n_hid):
+                if j + 1 < hid // n_hid:
+                    h_part(j + 1)
+                a_part(j)
+            down()
 
         @pl.when(step == HALF - 1)
         def _():
             load_w2(0).start()
+            load_w1(0).start()
             store_2(1).start()
+
+        @pl.when(step == STEPS - 1)
+        def _():
+            store_2(0).start()
 
         ticks(step, 2)
 
@@ -424,7 +490,9 @@
             acc1[dim_cols(j), :] += dot_tn(xb[slot, :, dim_cols(j)], dhb[...])
             return c
 
-        lax.fori_loop(0, dim // n_dim, up_part, 0, unroll=True)
+        @pl.when(step < STEPS - 1)
+        def _():
+            lax.fori_loop(0, dim // n_dim, up_part, 0, unroll=True)
 
         @pl.when(step == HALF - 1)
         def _():
@@ -434,17 +502,29 @@
 
     lax.fori_loop(0, STEPS, step_body, 0)
 
-    store_2(0).start()
-    store_1(0).start()
+    def last_part(j):
+        return pltpu.make_async_copy(acc1.at[dim_cols(j), :], dw1.at[0, dim_cols(j), :], misc.at[4])
+
+    def last_up(j, c):
+        acc1[dim_cols(j), :] += dot_tn(xb[(STEPS - 1) % 2, :, dim_cols(j)], dhb[...])
+
+        @pl.when(j > 0)
+        def _():
+            last_part(j - 1).wait()
+
+        last_part(j).start()
+        return c
+
+    lax.fori_loop(0, dim // n_dim, last_up, 0)
+    last_part(dim // n_dim - 1).wait()
     for mask in (1, 3, 5, 7):
-        wait_arrival(0, 3, 1, mask)
+        wait_on(buf_slice(0, 3, 1, mask), recv_at(0, 3, 1, mask))
     for make, cond in sent:
         if cond is None:
             make().wait_send()
         else:
             pl.when(cond())(lambda make=make: make().wait_send())
     store_2(0).wait()
-    store_1(0).wait()
 
 
 def backward(w_up, w_dn, x_sv, h_sv, g_in):
@@ -453,7 +533,8 @@
     part = tokens // N_TP
     hbm = pl.BlockSpec(memory_space=pl.ANY)
     outs = [
-        jax.ShapeDtypeStruct((2, tokens, dim), BF),
+        jax.ShapeDtypeStruct((tokens, dim), BF),
+        jax.ShapeDtypeStruct((tokens, dim), BF),
         jax.ShapeDtypeStruct((2, dim, hid), F32),
         jax.ShapeDtypeStruct((2, hid, dim), F32),
         jax.ShapeDtypeStruct((2, 3, tokens, dim), BF),
@@ -479,9 +560,9 @@
         dma((2,)),
         dma((2,)),
         dma((2 * OWN,)),
-        dma((6,)),
-        dma((128,)),
-        dma((176,)),
+        dma((12,)),
+        dma((256,)),
+        dma((288,)),
     ]
     return pl.pallas_call(
         kernel,
@@ -497,7 +578,7 @@
 
 def solution(mesh):
     def run_backward(w_up, w_down, x_saved, h_saved, grad_out):
-        grads, up, down, *_ = backward(w_up, w_down, x_saved[:, 0], h_saved[:, 0], grad_out[0])
-        return grads[:1], up, down
+        grad_in, _, up, down, *_ = backward(w_up, w_down, x_saved[:, 0], h_saved[:, 0], grad_out[0])
+        return grad_in[None], up, down
 
     return jax.shard_map(run_backward, mesh=mesh, in_specs=(P(None, None, "tp"), P(None, "tp", None), P(None, "dp", None, None), P(None, "dp", None, "tp"), P("dp", None, None)), out_specs=(P("dp", None, None), P(None, None, "tp"), P(None, "tp", None)), check_vma=False)

time: 762 us -> 708 us (0.929)
  Pallas kernels: 719 us -> 664 us
    pallas_call x1, Pallas kernels: 719 us -> 664 us  [backward(): pl.pallas_call(kernel, out_shape=outs, in_specs=[hbm] * 5, out_specs=[hbm...]
    unnamed x4 -> x5, local copies, waits for them, and re-layouts: 34.3 us -> 43.1 us
    slice x1 -> x0, local copies, waits for them, and re-layouts: 8.74 us -> none  [run_backward(): return (grads[:1], up, down)]
where the time goes in v2:
time: 708 us; the launch traced here: 707 us
  Pallas kernels  664 us (94%)
  local copies, waits for them, and re-layouts  43.1 us (6%)
    pallas_call x1, Pallas kernels, backward(): pl.pallas_call(kernel, out_shape=outs, in_specs=[hbm] * 5, out_specs=[hbm...  664 us
    unnamed x5, local copies, waits for them, and re-layouts  43.1 us

profile of v2, /device:TPU:0, one launch (start us, length us, event | category | flops | bytes accessed | tf_op | source)
XLA Modules:
  0.0 707.3 jit_solution(12628029830995523550)
XLA Ops:
  0.6 663.6 %backward.1 = (bf16[2048,2560]{1,0:T(8,128)(2,1)}, bf16[2048,2560]{1,0:T(8,128)(2,1)}, f32[2,2560,1280]{2,1,0:T(8,128)}, f32[2,1280,2560]{2,1,0:T(8,128)}, bf16[...) custom-call(bf16[2,2560,1280]{2,1,0:T(8,128)(2,1)} %refs_0_.1, ...), custom_call_target="tpu_custom_call" | custom-call | flops 429496729600 | tf_op jit(solution)/shard_map/backward/pallas_call | solution.py:567
  664.3 8.7 %copy.11 = bf16[1,2048,2560]{2,1,0:T(8,128)(2,1)} copy(bf16[1,2048,2560]{2,1,0:T(8,128)(2,1)} %bitcast.4) | data formatting | bytes 20971520
  673.0 0.0 copy-start
  673.0 18.6 %copy.12 = f32[2,2560,1280]{2,1,0:T(8,128)} copy(f32[2,2560,1280]{2,1,0:T(8,128)} %get-tuple-element.13) | data formatting | bytes 52428800
  691.6 6.5 copy-done
  698.1 9.3 %copy.13 = f32[2,1280,2560]{2,1,0:T(8,128)} copy(f32[2,1280,2560]{2,1,0:T(8,128)S(1)} %copy-done) | data formatting | bytes 52428800
Async XLA Ops:
  673.0 25.1 %copy-start = (f32[2,1280,2560]{2,1,0:T(8,128)S(1)}, f32[2,1280,2560]{2,1,0:T(8,128)}, u32[]{:S(2)}) copy-start(f32[2,1280,2560]{2,1,0:T(8,128)} %get-tuple-element.14) | copy-start | bytes 78643200

commit v3 on v2

--- a/solution.py
+++ b/solution.py
@@ -39,24 +39,24 @@
 SUB = 2
 KEYS = [(blk, slot, arr) for blk in (1, 0) for slot in range(4) for arr in range(2) if slot < 3 or arr == 1]
 ROUTES = (
-    ("x", "0103040d090c1214"),
-    ("dx", "0407080d0a100d14"),
-    ("dx", "0d151c1c17220f19"),
-    ("", "0c1114160d1b1522"),
-    ("d", "0e21162a162b3136"),
-    ("d", "152a2c2e2d2f2c35"),
-    ("x", "00002d2e2f324447"),
-    ("", "2d34323e3748434d"),
-    ("dx", "2e2e363a41454c51"),
-    ("dx", "3a514b5d565c435d"),
-    ("x", "3f52495a4c5b5366"),
-    ("d", "5769696e64726470"),
-    ("dx", "4d5f526953736b76"),
-    ("", "0000717d73777c7d"),
+    ("x", "0003090b080a0f11"),
+    ("d", "06080d0e0a160c0c"),
+    ("dx", "0e121414191b121a"),
+    ("", "0c120f16141c1b24"),
+    ("dx", "0f1f1e2a1d243036"),
+    ("d", "1829202e1e2f2d35"),
+    ("x", "00002a2d2c3a4647"),
+    ("", "2935363e3648404e"),
+    ("d", "2d3a394640494f54"),
+    ("d", "3a4f49574862425a"),
+    ("x", "3e54485d4d654f66"),
+    ("d", "5861626c6f716575"),
+    ("d", "4c5e526852706972"),
+    ("", "0000787c74787b7d"),
 )
-Z_ORDER = ((0, 0), (1, 0), (0, 6), (1, 6))
-X0_TICKS = (27, 4)
-COMBINE = {1: 26, 0: 94}
+Z_ORDER = ((0, 6), (0, 0), (1, 0), (1, 6))
+X0_TICKS = (29, 2)
+COMBINE = {1: 30, 0: 94}
 REDUCE = {1: 34, 0: 106}
 ROUTE = dict(zip(KEYS, ROUTES))
 PARTS = [(mask, sub) for mask in (0, 2, 4, 6) for sub in range(SUB)]
@@ -402,7 +402,19 @@
             for half in range(2):
                 wait_on(hb.at[halves(half), :], h_sem.at[half])
 
+        @pl.when(at >= OWN)
+        def _():
+            def h_part(j, c):
+                hb[:, hid_cols(j)] = dot_nn(xb[slot], w1[:, hid_cols(j)]).astype(BF)
+                return c
+
+            lax.fori_loop(0, hid // n_hid, h_part, 0, unroll=True)
+
         ticks(step, 1)
+
+        @pl.when(step == HALF - 1)
+        def _():
+            load_w1(0).start()
 
         @pl.when(step == HALF)
         def _():
@@ -412,37 +424,23 @@
 
         fetched(*g_dst())
 
-        def a_part(j):
+        def a_part(j, c):
             act, slope = gelu_parts(hb[:, hid_cols(j)].astype(F32))
             ab[:, hid_cols(j)] = act.astype(BF)
             dhb[:, hid_cols(j)] = (dot_nt(gb[...], w2[hid_cols(j), :]) * slope).astype(BF)
-
-
-        def h_part(j):
-            hb[:, hid_cols(j)] = dot_nn(xb[slot], w1[:, hid_cols(j)]).astype(BF)
-
-        def down():
-            acc2[...] += dot_tn(ab[...], gb[...])
-
-        @pl.when(is_own)
-        def _():
-            for j in range(hid // n_hid):
-                a_part(j)
-            down()
-
-        @pl.when(at >= OWN)
-        def _():
-            h_part(0)
-            for j in range(hid // n_hid):
-                if j + 1 < hid // n_hid:
-                    h_part(j + 1)
-                a_part(j)
-            down()
+            return c
+
+        lax.fori_loop(0, hid // n_hid, a_part, 0, unroll=True)
+
+        def down_part(j, c):
+            acc2[hid_cols(j), :] += dot_tn(ab[:, hid_cols(j)], gb[...])
+            return c
+
+        lax.fori_loop(0, hid // n_hid, down_part, 0, unroll=True)
 
         @pl.when(step == HALF - 1)
         def _():
             load_w2(0).start()
-            load_w1(0).start()
             store_2(1).start()
 
         @pl.when(step == STEPS - 1)

time: 708 us -> 709 us (level)
  no operation moved by 1% of the time
where the time goes in v3:
time: 709 us; the launch traced here: 708 us
  Pallas kernels  665 us (94%)
  local copies, waits for them, and re-layouts  43.1 us (6%)
    pallas_call x1, Pallas kernels, backward(): pl.pallas_call(kernel, out_shape=outs, in_specs=[hbm] * 5, out_specs=[hbm...  665 us
    unnamed x5, local copies, waits for them, and re-layouts  43.1 us

profile of v3, /device:TPU:0, one launch (start us, length us, event | category | flops | bytes accessed | tf_op | source)
XLA Modules:
  0.0 708.4 jit_solution(4696611823416601305)
XLA Ops:
  0.6 664.7 %backward.1 = (bf16[2048,2560]{1,0:T(8,128)(2,1)}, bf16[2048,2560]{1,0:T(8,128)(2,1)}, f32[2,2560,1280]{2,1,0:T(8,128)}, f32[2,1280,2560]{2,1,0:T(8,128)}, bf16[...) custom-call(bf16[2,2560,1280]{2,1,0:T(8,128)(2,1)} %refs_0_.1, ...), custom_call_target="tpu_custom_call" | custom-call | flops 429496729600 | tf_op jit(solution)/shard_map/backward/pallas_call | solution.py:565
  665.3 8.7 %copy.11 = bf16[1,2048,2560]{2,1,0:T(8,128)(2,1)} copy(bf16[1,2048,2560]{2,1,0:T(8,128)(2,1)} %bitcast.4) | data formatting | bytes 20971520
  674.1 0.0 copy-start
  674.1 18.6 %copy.12 = f32[2,2560,1280]{2,1,0:T(8,128)} copy(f32[2,2560,1280]{2,1,0:T(8,128)} %get-tuple-element.13) | data formatting | bytes 52428800
  692.6 6.5 copy-done
  699.1 9.3 %copy.13 = f32[2,1280,2560]{2,1,0:T(8,128)} copy(f32[2,1280,2560]{2,1,0:T(8,128)S(1)} %copy-done) | data formatting | bytes 52428800
Async XLA Ops:
  674.1 25.1 %copy-start = (f32[2,1280,2560]{2,1,0:T(8,128)S(1)}, f32[2,1280,2560]{2,1,0:T(8,128)}, u32[]{:S(2)}) copy-start(f32[2,1280,2560]{2,1,0:T(8,128)} %get-tuple-element.14) | copy-start | bytes 78643200
